TPU v7x, 32 devices: a whole 2x2x4 slice. The times are simulated.
32 devices in a mesh: gx: 8 (over y, x, core), gy: 4 (over z).
Axes of the slice: x: 2, y: 2, z: 4, core: 2. Of those that a mesh axis runs over, the one named last changes fastest.
Arguments:
- terminal: float32 [128, 2048], P('gx', 'gy'), may hold values from -15 to 15
- initial_density: float32 [128, 2048], P('gx', 'gy'), may hold values from 0.1 to 1
- density_guess: float32 [2, 128, 2048], P(None, 'gx', 'gy'), may hold values from 0.1 to 1
- diagonal: float32 [128, 2048], P('gx', 'gy'), may hold values from 0.1 to 2
Outputs:
- value_field: float32 [128, 2048], P('gx', 'gy')
- density_field: float32 [128, 2048], P('gx', 'gy')
All inputs are finite; a program needn't handle non-finite values.
Results may differ from a plain program's by a relative error of at most 0.00011.
Values sent between devices are 32-bit elements; how exact they have to be, the bound alone decides.
A program may use at most 64 MiB of HBM per device.

v0:
```python
import jax
import jax.numpy as jnp
from jax import lax
from jax.sharding import PartitionSpec as P

LEVELS = 2
STEPS = 3
inv_step = 0.5
coupling = 0.5


def padded_2(cells, sides, width):
    for axis, dim in sides:
        count = lax.axis_size(axis)
        ends = count - 1
        head = lax.slice_in_dim(cells, 0, width, axis=dim)
        tail = lax.slice_in_dim(cells, cells.shape[dim] - width, cells.shape[dim], axis=dim)
        cells = jnp.concatenate(
            [
                lax.ppermute(tail, axis, [(i, (i + 1) % count) for i in range(ends)]),
                cells,
                lax.ppermute(head, axis, [((i + 1) % count, i) for i in range(ends)]),
            ],
            axis=dim,
        )
    return cells


def apply_padded(padded, center, diagonal):
    beside = padded[2:, 1:-1] + padded[:-2, 1:-1] + padded[1:-1, 2:] + padded[1:-1, :-2]
    return (inv_step + diagonal) * center + (4.0 * center - beside)


def hamiltonian(padded):
    center = padded[1:-1, 1:-1]
    back_x = center - padded[:-2, 1:-1]
    ahead_x = padded[2:, 1:-1] - center
    back_y = center - padded[1:-1, :-2]
    ahead_y = padded[1:-1, 2:] - center
    return 0.5 * (
        jnp.maximum(back_x, 0.0) ** 2
        + jnp.minimum(ahead_x, 0.0) ** 2
        + jnp.maximum(back_y, 0.0) ** 2
        + jnp.minimum(ahead_y, 0.0) ** 2
    )


def divergence(pad_m, pad_u):
    m_mid = pad_m[1:-1, 1:-1]
    u_mid = pad_u[1:-1, 1:-1]
    speed_ahead = -(pad_u[2:, 1:-1] - u_mid)
    speed_back = -(u_mid - pad_u[:-2, 1:-1])
    flux_ahead = (
        jnp.maximum(speed_ahead, 0.0) * m_mid + jnp.minimum(speed_ahead, 0.0) * pad_m[2:, 1:-1]
    )
    flux_back = (
        jnp.maximum(speed_back, 0.0) * pad_m[:-2, 1:-1] + jnp.minimum(speed_back, 0.0) * m_mid
    )
    total = flux_ahead - flux_back
    speed_ahead = -(pad_u[1:-1, 2:] - u_mid)
    speed_back = -(u_mid - pad_u[1:-1, :-2])
    flux_ahead = (
        jnp.maximum(speed_ahead, 0.0) * m_mid + jnp.minimum(speed_ahead, 0.0) * pad_m[1:-1, 2:]
    )
    flux_back = (
        jnp.maximum(speed_back, 0.0) * pad_m[1:-1, :-2] + jnp.minimum(speed_back, 0.0) * m_mid
    )
    return total + flux_ahead - flux_back


def stencil(field, diagonal):
    padded = padded_2(field, (("gx", 0), ("gy", 1)), 1)
    return apply_padded(padded, field, diagonal)


def paired(resid, image):
    return lax.psum((jnp.sum(resid * resid), jnp.sum(resid * image)), ("gx", "gy"))


def solve(rhs, diagonal):
    answer = jnp.zeros_like(rhs)
    resid = rhs
    image = stencil(resid, diagonal)
    norm_now, product = paired(resid, image)
    alpha = norm_now / product
    direction = resid
    along = image
    for step in range(STEPS):
        answer = answer + alpha * direction
        if step + 1 < STEPS:
            resid = resid - alpha * along
            image = stencil(resid, diagonal)
            norm_next, product = paired(resid, image)
            ratio = norm_next / norm_now
            alpha = norm_next / (product - ratio * norm_next / alpha)
            direction = resid + ratio * direction
            along = image + ratio * along
            norm_now = norm_next
    return answer


def shards(terminal, initial_density, density_guess, diagonal):
    levels = [None] * LEVELS
    kept = [None] * (LEVELS + 1)
    later = terminal
    for level in reversed(range(LEVELS)):
        padded = padded_2(later, (("gx", 0), ("gy", 1)), 1)
        kept[level + 1] = padded
        rhs = inv_step * later - hamiltonian(padded) + coupling * density_guess[level]
        later = solve(rhs, diagonal)
        levels[level] = later
    density = initial_density
    for level in range(LEVELS):
        both = padded_2(jnp.stack([density, levels[level]]), (("gx", 1), ("gy", 2)), 1)
        pad_m = both[0]
        pad_u = both[1]
        rhs = inv_step * density - divergence(pad_m, pad_u)
        density = solve(rhs, diagonal)
    return (levels[0], density)


def solution(mesh):
    placed = (P("gx", "gy"), P("gx", "gy"), P(None, "gx", "gy"), P("gx", "gy"))
    return jax.shard_map(
        shards,
        mesh=mesh,
        in_specs=placed,
        out_specs=(P("gx", "gy"), P("gx", "gy")),
        check_vma=False,
    )
```

profile of v0, /device:TPU:0, one launch (start us, length us, event | category | flops | bytes accessed | tf_op | source)
XLA Modules:
  0.0 794.6 jit_solution(6539389510848766580)
XLA Ops:
  27.9 4.5 collective-permute-start.7
  34.6 42.7 %all-reduce.11 = (f32[]{:T(128)}, f32[]{:T(128)}) all-reduce(f32[]{:T(128)} %get-tuple-element.25, f32[]{:T(128)} %get-tuple-element.24), channel_id=1, replica_groups=mesh['gx'=8,'gy'=4] {'gx','gy'}, use_global_device_ids=true, to_apply=%region_1.0 | all-reduce | flops 2 | bytes 16 | tf_op jit(solution)/shard_map/psum | solution.py:77
  86.9 4.5 collective-permute-start.11
  93.6 42.6 %all-reduce.10 = (f32[]{:T(128)}, f32[]{:T(128)}) all-reduce(f32[]{:T(128)} %get-tuple-element.23, f32[]{:T(128)} %get-tuple-element.22), channel_id=1, replica_groups=mesh['gx'=8,'gy'=4] {'gx','gy'}, use_global_device_ids=true, to_apply=%region_5.0 | all-reduce | flops 2 | bytes 16 | tf_op jit(solution)/shard_map/psum | solution.py:77
  149.1 4.5 collective-permute-start.15
  155.8 41.8 %all-reduce.9 = (f32[]{:T(128)}, f32[]{:T(128)}) all-reduce(f32[]{:T(128)} %get-tuple-element.21, f32[]{:T(128)} %get-tuple-element.20), channel_id=1, replica_groups=mesh['gx'=8,'gy'=4] {'gx','gy'}, use_global_device_ids=true, to_apply=%region_9.0 | all-reduce | flops 2 | bytes 16 | tf_op jit(solution)/shard_map/psum | solution.py:77
  225.6 4.5 collective-permute-start.23
  232.2 42.6 %all-reduce.8 = (f32[]{:T(128)}, f32[]{:T(128)}) all-reduce(f32[]{:T(128)} %get-tuple-element.19, f32[]{:T(128)} %get-tuple-element.18), channel_id=1, replica_groups=mesh['gx'=8,'gy'=4] {'gx','gy'}, use_global_device_ids=true, to_apply=%region_13.0 | all-reduce | flops 2 | bytes 16 | tf_op jit(solution)/shard_map/psum | solution.py:77
  284.4 4.5 collective-permute-start.27
  291.2 42.5 %all-reduce.7 = (f32[]{:T(128)}, f32[]{:T(128)}) all-reduce(f32[]{:T(128)} %get-tuple-element.17, f32[]{:T(128)} %get-tuple-element.16), channel_id=1, replica_groups=mesh['gx'=8,'gy'=4] {'gx','gy'}, use_global_device_ids=true, to_apply=%region_17.0 | all-reduce | flops 2 | bytes 16 | tf_op jit(solution)/shard_map/psum | solution.py:77
  346.5 4.5 collective-permute-start.31
  353.2 41.9 %all-reduce.6 = (f32[]{:T(128)}, f32[]{:T(128)}) all-reduce(f32[]{:T(128)} %get-tuple-element.15, f32[]{:T(128)} %get-tuple-element.14), channel_id=1, replica_groups=mesh['gx'=8,'gy'=4] {'gx','gy'}, use_global_device_ids=true, to_apply=%region_21.0 | all-reduce | flops 2 | bytes 16 | tf_op jit(solution)/shard_map/psum | solution.py:77
  423.4 4.5 collective-permute-start.39
  430.0 42.7 %all-reduce.5 = (f32[]{:T(128)}, f32[]{:T(128)}) all-reduce(f32[]{:T(128)} %get-tuple-element.13, f32[]{:T(128)} %get-tuple-element.12), channel_id=1, replica_groups=mesh['gx'=8,'gy'=4] {'gx','gy'}, use_global_device_ids=true, to_apply=%region_25.0 | all-reduce | flops 2 | bytes 16 | tf_op jit(solution)/shard_map/psum | solution.py:77
  482.4 4.5 collective-permute-start.43
  489.1 42.6 %all-reduce.4 = (f32[]{:T(128)}, f32[]{:T(128)}) all-reduce(f32[]{:T(128)} %get-tuple-element.11, f32[]{:T(128)} %get-tuple-element.10), channel_id=1, replica_groups=mesh['gx'=8,'gy'=4] {'gx','gy'}, use_global_device_ids=true, to_apply=%region_29.0 | all-reduce | flops 2 | bytes 16 | tf_op jit(solution)/shard_map/psum | solution.py:77
  544.5 4.5 collective-permute-start.47
  551.2 41.8 %all-reduce.3 = (f32[]{:T(128)}, f32[]{:T(128)}) all-reduce(f32[]{:T(128)} %get-tuple-element.9, f32[]{:T(128)} %get-tuple-element.8), channel_id=1, replica_groups=mesh['gx'=8,'gy'=4] {'gx','gy'}, use_global_device_ids=true, to_apply=%region_33.0 | all-reduce | flops 2 | bytes 16 | tf_op jit(solution)/shard_map/psum | solution.py:77
  620.5 4.5 collective-permute-start.55
  627.1 42.8 %all-reduce.2 = (f32[]{:T(128)}, f32[]{:T(128)}) all-reduce(f32[]{:T(128)} %get-tuple-element.7, f32[]{:T(128)} %get-tuple-element.6), channel_id=1, replica_groups=mesh['gx'=8,'gy'=4] {'gx','gy'}, use_global_device_ids=true, to_apply=%region_37.0 | all-reduce | flops 2 | bytes 16 | tf_op jit(solution)/shard_map/psum | solution.py:77
  679.5 4.5 collective-permute-start.59
  686.3 42.5 %all-reduce.1 = (f32[]{:T(128)}, f32[]{:T(128)}) all-reduce(f32[]{:T(128)} %get-tuple-element.5, f32[]{:T(128)} %get-tuple-element.4), channel_id=1, replica_groups=mesh['gx'=8,'gy'=4] {'gx','gy'}, use_global_device_ids=true, to_apply=%region_41.0 | all-reduce | flops 2 | bytes 16 | tf_op jit(solution)/shard_map/psum | solution.py:77
  741.6 4.5 collective-permute-start.63
  748.2 41.8 %all-reduce = (f32[]{:T(128)}, f32[]{:T(128)}) all-reduce(f32[]{:T(128)} %get-tuple-element.3, f32[]{:T(128)} %get-tuple-element.2), channel_id=1, replica_groups=mesh['gx'=8,'gy'=4] {'gx','gy'}, use_global_device_ids=true, to_apply=%region_45.0 | all-reduce | flops 2 | bytes 16 | tf_op jit(solution)/shard_map/psum | solution.py:77
  (190 shorter events, 191.0 us)
Async XLA Ops:
  26.6 5.8 collective-permute-start.6
  27.9 5.9 collective-permute-start.7
  85.6 5.8 collective-permute-start.10
  86.9 5.9 collective-permute-start.11
  147.8 5.8 collective-permute-start.14
  149.1 5.9 collective-permute-start.15
  224.3 5.8 collective-permute-start.22
  225.6 5.9 collective-permute-start.23
  283.1 5.8 collective-permute-start.26
  284.4 5.9 collective-permute-start.27
  345.2 5.8 collective-permute-start.30
  346.5 5.9 collective-permute-start.31
  422.1 5.8 collective-permute-start.38
  423.4 5.9 collective-permute-start.39
  481.1 5.8 collective-permute-start.42
  482.4 5.9 collective-permute-start.43
  543.2 5.8 collective-permute-start.46
  544.5 5.9 collective-permute-start.47
  619.2 5.8 collective-permute-start.54
  620.5 5.9 collective-permute-start.55
  678.3 5.8 collective-permute-start.58
  679.5 5.9 collective-permute-start.59
  740.3 5.8 collective-permute-start.62
  741.6 5.9 collective-permute-start.63
  (45 other events, 230.0 us)
where the time goes:
time: 799 us; the launch traced here: 795 us
  blocking collectives  508 us (64%)
  starting transfers between devices  135 us (17%)
  waiting for transfers between devices  95.6 us (12%)
  between operations  40.8 us (5%)
  other arithmetic  13.3 us (2%)
    psum x12, blocking collectives, paired(): lax.psum((jnp.sum(resid * resid), jnp.sum(resid * image)), ('gx', 'gy'))  508 us
    ppermute x32, starting transfers between devices, padded_2(): lax.ppermute(tail, axis, [(i, (i + 1) % count) for i in range(ends)])  93.9 us
    ppermute x32, waiting for transfers between devices, padded_2(): lax.ppermute(head, axis, [((i + 1) % count, i) for i in range(ends)])  78.5 us
    ppermute x32, starting transfers between devices, padded_2(): lax.ppermute(head, axis, [((i + 1) % count, i) for i in range(ends)])  41.2 us
    ppermute x32, waiting for transfers between devices, padded_2(): lax.ppermute(tail, axis, [(i, (i + 1) % count) for i in range(ends)])  17.1 us
  transfers between devices with their start and end apart: 64, of which 36 were waited for; matrix products, arithmetic and copies ran while one was open for 0% of the time, Pallas kernels for 0%

commit v1 on v0

--- a/solution.py
+++ b/solution.py
@@ -7,6 +7,11 @@
 STEPS = 3
 inv_step = 0.5
 coupling = 0.5
+
+
+def by_each_axis(x, one, other):
+    inner = lax.psum(x, one)
+    return lax.psum(inner, other)
 
 
 def padded_2(cells, sides, width):
@@ -74,7 +79,7 @@
 
 
 def paired(resid, image):
-    return lax.psum((jnp.sum(resid * resid), jnp.sum(resid * image)), ("gx", "gy"))
+    return by_each_axis((jnp.sum(resid * resid), jnp.sum(resid * image)), "gy", "gx")
 
 
 def solve(rhs, diagonal):

time: 799 us -> 587 us (0.73)
  blocking collectives: 508 us -> 296 us
    psum x12 -> x24, blocking collectives: 508 us -> 296 us  [the longest x12 157 us: by_each_axis(): return lax.psum(inner, other)]
where the time goes in v1:
time: 587 us; the launch traced here: 582 us
  blocking collectives  296 us (50%)
  starting transfers between devices  140 us (24%)
  waiting for transfers between devices  91.2 us (16%)
  between operations  40.5 us (7%)
  other arithmetic  13.4 us (2%)
    psum x12, blocking collectives, by_each_axis(): return lax.psum(inner, other)  157 us
    psum x12, blocking collectives, by_each_axis(): inner = lax.psum(x, one)  138 us
    ppermute x32, starting transfers between devices, padded_2(): lax.ppermute(tail, axis, [(i, (i + 1) % count) for i in range(ends)])  98.9 us
    ppermute x32, waiting for transfers between devices, padded_2(): lax.ppermute(head, axis, [((i + 1) % count, i) for i in range(ends)])  74 us
    ppermute x32, starting transfers between devices, padded_2(): lax.ppermute(head, axis, [((i + 1) % count, i) for i in range(ends)])  41.2 us
    ppermute x32, waiting for transfers between devices, padded_2(): lax.ppermute(tail, axis, [(i, (i + 1) % count) for i in range(ends)])  17.1 us
  transfers between devices with their start and end apart: 64, of which 36 were waited for; matrix products, arithmetic and copies ran while one was open for 0% of the time, Pallas kernels for 0%

profile of v1, /device:TPU:0, one launch (start us, length us, event | category | flops | bytes accessed | tf_op | source)
XLA Modules:
  0.0 582.4 jit_solution(13555412365259933945)
XLA Ops:
  34.6 13.3 %all-reduce.23 = (f32[]{:T(128)}, f32[]{:T(128)}) all-reduce(f32[]{:T(128)} %get-tuple-element.25, f32[]{:T(128)} %get-tuple-element.24), channel_id=1, replica_groups=mesh['gx'=8,'gy'=4] {'gy'}, use_global_device_ids=true, to_apply=%region_1.0 | all-reduce | flops 2 | bytes 16 | tf_op jit(solution)/shard_map/psum | solution.py:13
  47.9 12.6 %all-reduce.11 = (f32[]{:T(128)}, f32[]{:T(128)}) all-reduce(f32[]{:T(128)} %get-tuple-element.72, f32[]{:T(128)} %get-tuple-element.73), channel_id=1, replica_groups=mesh['gx'=8,'gy'=4] {'gx'}, use_global_device_ids=true, to_apply=%region_2.0 | all-reduce | flops 2 | bytes 16 | tf_op jit(solution)/shard_map/psum | solution.py:14
  76.2 11.4 %all-reduce.22 = (f32[]{:T(128)}, f32[]{:T(128)}) all-reduce(f32[]{:T(128)} %get-tuple-element.23, f32[]{:T(128)} %get-tuple-element.22), channel_id=1, replica_groups=mesh['gx'=8,'gy'=4] {'gy'}, use_global_device_ids=true, to_apply=%region_7.0 | all-reduce | flops 2 | bytes 16 | tf_op jit(solution)/shard_map/psum | solution.py:13
  87.6 13.3 %all-reduce.10 = (f32[]{:T(128)}, f32[]{:T(128)}) all-reduce(f32[]{:T(128)} %get-tuple-element.70, f32[]{:T(128)} %get-tuple-element.71), channel_id=1, replica_groups=mesh['gx'=8,'gy'=4] {'gx'}, use_global_device_ids=true, to_apply=%region_8.0 | all-reduce | flops 2 | bytes 16 | tf_op jit(solution)/shard_map/psum | solution.py:14
  120.5 11.3 %all-reduce.21 = (f32[]{:T(128)}, f32[]{:T(128)}) all-reduce(f32[]{:T(128)} %get-tuple-element.21, f32[]{:T(128)} %get-tuple-element.20), channel_id=1, replica_groups=mesh['gx'=8,'gy'=4] {'gy'}, use_global_device_ids=true, to_apply=%region_13.0 | all-reduce | flops 2 | bytes 16 | tf_op jit(solution)/shard_map/psum | solution.py:13
  131.8 13.3 %all-reduce.9 = (f32[]{:T(128)}, f32[]{:T(128)}) all-reduce(f32[]{:T(128)} %get-tuple-element.68, f32[]{:T(128)} %get-tuple-element.69), channel_id=1, replica_groups=mesh['gx'=8,'gy'=4] {'gx'}, use_global_device_ids=true, to_apply=%region_14.0 | all-reduce | flops 2 | bytes 16 | tf_op jit(solution)/shard_map/psum | solution.py:14
  179.6 11.4 %all-reduce.20 = (f32[]{:T(128)}, f32[]{:T(128)}) all-reduce(f32[]{:T(128)} %get-tuple-element.19, f32[]{:T(128)} %get-tuple-element.18), channel_id=1, replica_groups=mesh['gx'=8,'gy'=4] {'gy'}, use_global_device_ids=true, to_apply=%region_19.0 | all-reduce | flops 2 | bytes 16 | tf_op jit(solution)/shard_map/psum | solution.py:13
  191.0 12.8 %all-reduce.8 = (f32[]{:T(128)}, f32[]{:T(128)}) all-reduce(f32[]{:T(128)} %get-tuple-element.66, f32[]{:T(128)} %get-tuple-element.67), channel_id=1, replica_groups=mesh['gx'=8,'gy'=4] {'gx'}, use_global_device_ids=true, to_apply=%region_20.0 | all-reduce | flops 2 | bytes 16 | tf_op jit(solution)/shard_map/psum | solution.py:14
  220.1 11.4 %all-reduce.19 = (f32[]{:T(128)}, f32[]{:T(128)}) all-reduce(f32[]{:T(128)} %get-tuple-element.17, f32[]{:T(128)} %get-tuple-element.16), channel_id=1, replica_groups=mesh['gx'=8,'gy'=4] {'gy'}, use_global_device_ids=true, to_apply=%region_25.0 | all-reduce | flops 2 | bytes 16 | tf_op jit(solution)/shard_map/psum | solution.py:13
  231.4 13.3 %all-reduce.7 = (f32[]{:T(128)}, f32[]{:T(128)}) all-reduce(f32[]{:T(128)} %get-tuple-element.64, f32[]{:T(128)} %get-tuple-element.65), channel_id=1, replica_groups=mesh['gx'=8,'gy'=4] {'gx'}, use_global_device_ids=true, to_apply=%region_26.0 | all-reduce | flops 2 | bytes 16 | tf_op jit(solution)/shard_map/psum | solution.py:14
  264.4 11.3 %all-reduce.18 = (f32[]{:T(128)}, f32[]{:T(128)}) all-reduce(f32[]{:T(128)} %get-tuple-element.15, f32[]{:T(128)} %get-tuple-element.14), channel_id=1, replica_groups=mesh['gx'=8,'gy'=4] {'gy'}, use_global_device_ids=true, to_apply=%region_31.0 | all-reduce | flops 2 | bytes 16 | tf_op jit(solution)/shard_map/psum | solution.py:13
  275.7 13.3 %all-reduce.6 = (f32[]{:T(128)}, f32[]{:T(128)}) all-reduce(f32[]{:T(128)} %get-tuple-element.62, f32[]{:T(128)} %get-tuple-element.63), channel_id=1, replica_groups=mesh['gx'=8,'gy'=4] {'gx'}, use_global_device_ids=true, to_apply=%region_32.0 | all-reduce | flops 2 | bytes 16 | tf_op jit(solution)/shard_map/psum | solution.py:14
  324.6 11.4 %all-reduce.17 = (f32[]{:T(128)}, f32[]{:T(128)}) all-reduce(f32[]{:T(128)} %get-tuple-element.13, f32[]{:T(128)} %get-tuple-element.12), channel_id=1, replica_groups=mesh['gx'=8,'gy'=4] {'gy'}, use_global_device_ids=true, to_apply=%region_37.0 | all-reduce | flops 2 | bytes 16 | tf_op jit(solution)/shard_map/psum | solution.py:13
  335.9 12.9 %all-reduce.5 = (f32[]{:T(128)}, f32[]{:T(128)}) all-reduce(f32[]{:T(128)} %get-tuple-element.60, f32[]{:T(128)} %get-tuple-element.61), channel_id=1, replica_groups=mesh['gx'=8,'gy'=4] {'gx'}, use_global_device_ids=true, to_apply=%region_38.0 | all-reduce | flops 2 | bytes 16 | tf_op jit(solution)/shard_map/psum | solution.py:14
  365.1 11.4 %all-reduce.16 = (f32[]{:T(128)}, f32[]{:T(128)}) all-reduce(f32[]{:T(128)} %get-tuple-element.11, f32[]{:T(128)} %get-tuple-element.10), channel_id=1, replica_groups=mesh['gx'=8,'gy'=4] {'gy'}, use_global_device_ids=true, to_apply=%region_43.0 | all-reduce | flops 2 | bytes 16 | tf_op jit(solution)/shard_map/psum | solution.py:13
  376.5 13.3 %all-reduce.4 = (f32[]{:T(128)}, f32[]{:T(128)}) all-reduce(f32[]{:T(128)} %get-tuple-element.58, f32[]{:T(128)} %get-tuple-element.59), channel_id=1, replica_groups=mesh['gx'=8,'gy'=4] {'gx'}, use_global_device_ids=true, to_apply=%region_44.0 | all-reduce | flops 2 | bytes 16 | tf_op jit(solution)/shard_map/psum | solution.py:14
  409.2 11.4 %all-reduce.15 = (f32[]{:T(128)}, f32[]{:T(128)}) all-reduce(f32[]{:T(128)} %get-tuple-element.9, f32[]{:T(128)} %get-tuple-element.8), channel_id=1, replica_groups=mesh['gx'=8,'gy'=4] {'gy'}, use_global_device_ids=true, to_apply=%region_49.0 | all-reduce | flops 2 | bytes 16 | tf_op jit(solution)/shard_map/psum | solution.py:13
  420.6 13.3 %all-reduce.3 = (f32[]{:T(128)}, f32[]{:T(128)}) all-reduce(f32[]{:T(128)} %get-tuple-element.56, f32[]{:T(128)} %get-tuple-element.57), channel_id=1, replica_groups=mesh['gx'=8,'gy'=4] {'gx'}, use_global_device_ids=true, to_apply=%region_50.0 | all-reduce | flops 2 | bytes 16 | tf_op jit(solution)/shard_map/psum | solution.py:14
  468.6 11.4 %all-reduce.14 = (f32[]{:T(128)}, f32[]{:T(128)}) all-reduce(f32[]{:T(128)} %get-tuple-element.7, f32[]{:T(128)} %get-tuple-element.6), channel_id=1, replica_groups=mesh['gx'=8,'gy'=4] {'gy'}, use_global_device_ids=true, to_apply=%region_55.0 | all-reduce | flops 2 | bytes 16 | tf_op jit(solution)/shard_map/psum | solution.py:13
  480.0 12.9 %all-reduce.2 = (f32[]{:T(128)}, f32[]{:T(128)}) all-reduce(f32[]{:T(128)} %get-tuple-element.54, f32[]{:T(128)} %get-tuple-element.55), channel_id=1, replica_groups=mesh['gx'=8,'gy'=4] {'gx'}, use_global_device_ids=true, to_apply=%region_56.0 | all-reduce | flops 2 | bytes 16 | tf_op jit(solution)/shard_map/psum | solution.py:14
  509.2 11.4 %all-reduce.13 = (f32[]{:T(128)}, f32[]{:T(128)}) all-reduce(f32[]{:T(128)} %get-tuple-element.5, f32[]{:T(128)} %get-tuple-element.4), channel_id=1, replica_groups=mesh['gx'=8,'gy'=4] {'gy'}, use_global_device_ids=true, to_apply=%region_61.0 | all-reduce | flops 2 | bytes 16 | tf_op jit(solution)/shard_map/psum | solution.py:13
  520.6 13.3 %all-reduce.1 = (f32[]{:T(128)}, f32[]{:T(128)}) all-reduce(f32[]{:T(128)} %get-tuple-element.52, f32[]{:T(128)} %get-tuple-element.53), channel_id=1, replica_groups=mesh['gx'=8,'gy'=4] {'gx'}, use_global_device_ids=true, to_apply=%region_62.0 | all-reduce | flops 2 | bytes 16 | tf_op jit(solution)/shard_map/psum | solution.py:14
  553.3 11.4 %all-reduce.12 = (f32[]{:T(128)}, f32[]{:T(128)}) all-reduce(f32[]{:T(128)} %get-tuple-element.3, f32[]{:T(128)} %get-tuple-element.2), channel_id=1, replica_groups=mesh['gx'=8,'gy'=4] {'gy'}, use_global_device_ids=true, to_apply=%region_67.0 | all-reduce | flops 2 | bytes 16 | tf_op jit(solution)/shard_map/psum | solution.py:13
  564.7 13.3 %all-reduce = (f32[]{:T(128)}, f32[]{:T(128)}) all-reduce(f32[]{:T(128)} %get-tuple-element.50, f32[]{:T(128)} %get-tuple-element.51), channel_id=1, replica_groups=mesh['gx'=8,'gy'=4] {'gx'}, use_global_device_ids=true, to_apply=%region_68.0 | all-reduce | flops 2 | bytes 16 | tf_op jit(solution)/shard_map/psum | solution.py:14
  (202 shorter events, 246.3 us)
Async XLA Ops:
  26.6 5.8 %collective-permute-start.6 = (f32[18,1]{1,0:T(8,128)S(1)}, f32[18,1]{1,0:T(8,128)S(1)}, u32[]{:S(2)}, u32[]{:S(2)}) collective-permute-start(f32[18,1]{1,0:T(8,128)S(1)} %get-tuple-element.114), channel_id=1, source_target_pairs={{1,0},{2,1},{3,2},{5,4},{6,5},{7,6},{9,8},{10,9},{11,10},{13,12},{... | collective-permute-start | bytes 224 | tf_op jit(solution)/shard_map/ppermute | solution.py:27
  27.9 5.9 %collective-permute-start.7 = (f32[18,1]{1,0:T(8,128)S(1)}, f32[18,1]{1,0:T(8,128)S(1)}, u32[]{:S(2)}, u32[]{:S(2)}) collective-permute-start(f32[18,1]{1,0:T(8,128)S(1)} %get-tuple-element.115), channel_id=1, source_target_pairs={{0,1},{1,2},{2,3},{4,5},{5,6},{6,7},{8,9},{9,10},{10,11},{12,13},{... | collective-permute-start | bytes 224 | tf_op jit(solution)/shard_map/ppermute | solution.py:25
  68.2 5.8 %collective-permute-start.10 = (f32[18,1]{1,0:T(8,128)S(1)}, f32[18,1]{1,0:T(8,128)S(1)}, u32[]{:S(2)}, u32[]{:S(2)}) collective-permute-start(f32[18,1]{1,0:T(8,128)S(1)} %get-tuple-element.112), channel_id=1, source_target_pairs={{1,0},{2,1},{3,2},{5,4},{6,5},{7,6},{9,8},{10,9},{11,10},{13,12},{... | collective-permute-start | bytes 224 | tf_op jit(solution)/shard_map/ppermute | solution.py:27
  69.5 5.9 %collective-permute-start.11 = (f32[18,1]{1,0:T(8,128)S(1)}, f32[18,1]{1,0:T(8,128)S(1)}, u32[]{:S(2)}, u32[]{:S(2)}) collective-permute-start(f32[18,1]{1,0:T(8,128)S(1)} %get-tuple-element.113), channel_id=1, source_target_pairs={{0,1},{1,2},{2,3},{4,5},{5,6},{6,7},{8,9},{9,10},{10,11},{12,13},{... | collective-permute-start | bytes 224 | tf_op jit(solution)/shard_map/ppermute | solution.py:25
  112.6 5.8 %collective-permute-start.14 = (f32[18,1]{1,0:T(8,128)S(1)}, f32[18,1]{1,0:T(8,128)S(1)}, u32[]{:S(2)}, u32[]{:S(2)}) collective-permute-start(f32[18,1]{1,0:T(8,128)S(1)} %get-tuple-element.110), channel_id=1, source_target_pairs={{1,0},{2,1},{3,2},{5,4},{6,5},{7,6},{9,8},{10,9},{11,10},{13,12},{... | collective-permute-start | bytes 224 | tf_op jit(solution)/shard_map/ppermute | solution.py:27
  113.9 5.9 %collective-permute-start.15 = (f32[18,1]{1,0:T(8,128)S(1)}, f32[18,1]{1,0:T(8,128)S(1)}, u32[]{:S(2)}, u32[]{:S(2)}) collective-permute-start(f32[18,1]{1,0:T(8,128)S(1)} %get-tuple-element.111), channel_id=1, source_target_pairs={{0,1},{1,2},{2,3},{4,5},{5,6},{6,7},{8,9},{9,10},{10,11},{12,13},{... | collective-permute-start | bytes 224 | tf_op jit(solution)/shard_map/ppermute | solution.py:25
  171.6 5.8 %collective-permute-start.22 = (f32[18,1]{1,0:T(8,128)S(1)}, f32[18,1]{1,0:T(8,128)S(1)}, u32[]{:S(2)}, u32[]{:S(2)}) collective-permute-start(f32[18,1]{1,0:T(8,128)S(1)} %get-tuple-element.106), channel_id=1, source_target_pairs={{1,0},{2,1},{3,2},{5,4},{6,5},{7,6},{9,8},{10,9},{11,10},{13,12},{... | collective-permute-start | bytes 224 | tf_op jit(solution)/shard_map/ppermute | solution.py:27
  172.9 5.9 %collective-permute-start.23 = (f32[18,1]{1,0:T(8,128)S(1)}, f32[18,1]{1,0:T(8,128)S(1)}, u32[]{:S(2)}, u32[]{:S(2)}) collective-permute-start(f32[18,1]{1,0:T(8,128)S(1)} %get-tuple-element.107), channel_id=1, source_target_pairs={{0,1},{1,2},{2,3},{4,5},{5,6},{6,7},{8,9},{9,10},{10,11},{12,13},{... | collective-permute-start | bytes 224 | tf_op jit(solution)/shard_map/ppermute | solution.py:25
  212.1 5.8 %collective-permute-start.26 = (f32[18,1]{1,0:T(8,128)S(1)}, f32[18,1]{1,0:T(8,128)S(1)}, u32[]{:S(2)}, u32[]{:S(2)}) collective-permute-start(f32[18,1]{1,0:T(8,128)S(1)} %get-tuple-element.104), channel_id=1, source_target_pairs={{1,0},{2,1},{3,2},{5,4},{6,5},{7,6},{9,8},{10,9},{11,10},{13,12},{... | collective-permute-start | bytes 224 | tf_op jit(solution)/shard_map/ppermute | solution.py:27
  213.4 5.9 %collective-permute-start.27 = (f32[18,1]{1,0:T(8,128)S(1)}, f32[18,1]{1,0:T(8,128)S(1)}, u32[]{:S(2)}, u32[]{:S(2)}) collective-permute-start(f32[18,1]{1,0:T(8,128)S(1)} %get-tuple-element.105), channel_id=1, source_target_pairs={{0,1},{1,2},{2,3},{4,5},{5,6},{6,7},{8,9},{9,10},{10,11},{12,13},{... | collective-permute-start | bytes 224 | tf_op jit(solution)/shard_map/ppermute | solution.py:25
  256.4 5.8 %collective-permute-start.30 = (f32[18,1]{1,0:T(8,128)S(1)}, f32[18,1]{1,0:T(8,128)S(1)}, u32[]{:S(2)}, u32[]{:S(2)}) collective-permute-start(f32[18,1]{1,0:T(8,128)S(1)} %get-tuple-element.102), channel_id=1, source_target_pairs={{1,0},{2,1},{3,2},{5,4},{6,5},{7,6},{9,8},{10,9},{11,10},{13,12},{... | collective-permute-start | bytes 224 | tf_op jit(solution)/shard_map/ppermute | solution.py:27
  257.7 5.9 %collective-permute-start.31 = (f32[18,1]{1,0:T(8,128)S(1)}, f32[18,1]{1,0:T(8,128)S(1)}, u32[]{:S(2)}, u32[]{:S(2)}) collective-permute-start(f32[18,1]{1,0:T(8,128)S(1)} %get-tuple-element.103), channel_id=1, source_target_pairs={{0,1},{1,2},{2,3},{4,5},{5,6},{6,7},{8,9},{9,10},{10,11},{12,13},{... | collective-permute-start | bytes 224 | tf_op jit(solution)/shard_map/ppermute | solution.py:25
  316.5 5.8 %collective-permute-start.38 = (f32[18,1]{1,0:T(8,128)S(1)}, f32[18,1]{1,0:T(8,128)S(1)}, u32[]{:S(2)}, u32[]{:S(2)}) collective-permute-start(f32[18,1]{1,0:T(8,128)S(1)} %get-tuple-element.100), channel_id=1, source_target_pairs={{1,0},{2,1},{3,2},{5,4},{6,5},{7,6},{9,8},{10,9},{11,10},{13,12},{... | collective-permute-start | bytes 224 | tf_op jit(solution)/shard_map/ppermute | solution.py:27
  317.8 5.9 %collective-permute-start.39 = (f32[18,1]{1,0:T(8,128)S(1)}, f32[18,1]{1,0:T(8,128)S(1)}, u32[]{:S(2)}, u32[]{:S(2)}) collective-permute-start(f32[18,1]{1,0:T(8,128)S(1)} %get-tuple-element.101), channel_id=1, source_target_pairs={{0,1},{1,2},{2,3},{4,5},{5,6},{6,7},{8,9},{9,10},{10,11},{12,13},{... | collective-permute-start | bytes 224 | tf_op jit(solution)/shard_map/ppermute | solution.py:25
  357.2 5.8 %collective-permute-start.42 = (f32[18,1]{1,0:T(8,128)S(1)}, f32[18,1]{1,0:T(8,128)S(1)}, u32[]{:S(2)}, u32[]{:S(2)}) collective-permute-start(f32[18,1]{1,0:T(8,128)S(1)} %get-tuple-element.98), channel_id=1, source_target_pairs={{1,0},{2,1},{3,2},{5,4},{6,5},{7,6},{9,8},{10,9},{11,10},{13,12},{... | collective-permute-start | bytes 224 | tf_op jit(solution)/shard_map/ppermute | solution.py:27
  358.5 5.9 %collective-permute-start.43 = (f32[18,1]{1,0:T(8,128)S(1)}, f32[18,1]{1,0:T(8,128)S(1)}, u32[]{:S(2)}, u32[]{:S(2)}) collective-permute-start(f32[18,1]{1,0:T(8,128)S(1)} %get-tuple-element.99), channel_id=1, source_target_pairs={{0,1},{1,2},{2,3},{4,5},{5,6},{6,7},{8,9},{9,10},{10,11},{12,13},{... | collective-permute-start | bytes 224 | tf_op jit(solution)/shard_map/ppermute | solution.py:25
  401.3 5.8 %collective-permute-start.46 = (f32[18,1]{1,0:T(8,128)S(1)}, f32[18,1]{1,0:T(8,128)S(1)}, u32[]{:S(2)}, u32[]{:S(2)}) collective-permute-start(f32[18,1]{1,0:T(8,128)S(1)} %get-tuple-element.96), channel_id=1, source_target_pairs={{1,0},{2,1},{3,2},{5,4},{6,5},{7,6},{9,8},{10,9},{11,10},{13,12},{... | collective-permute-start | bytes 224 | tf_op jit(solution)/shard_map/ppermute | solution.py:27
  402.6 5.9 %collective-permute-start.47 = (f32[18,1]{1,0:T(8,128)S(1)}, f32[18,1]{1,0:T(8,128)S(1)}, u32[]{:S(2)}, u32[]{:S(2)}) collective-permute-start(f32[18,1]{1,0:T(8,128)S(1)} %get-tuple-element.97), channel_id=1, source_target_pairs={{0,1},{1,2},{2,3},{4,5},{5,6},{6,7},{8,9},{9,10},{10,11},{12,13},{... | collective-permute-start | bytes 224 | tf_op jit(solution)/shard_map/ppermute | solution.py:25
  460.6 5.8 %collective-permute-start.54 = (f32[18,1]{1,0:T(8,128)S(1)}, f32[18,1]{1,0:T(8,128)S(1)}, u32[]{:S(2)}, u32[]{:S(2)}) collective-permute-start(f32[18,1]{1,0:T(8,128)S(1)} %get-tuple-element.94), channel_id=1, source_target_pairs={{1,0},{2,1},{3,2},{5,4},{6,5},{7,6},{9,8},{10,9},{11,10},{13,12},{... | collective-permute-start | bytes 224 | tf_op jit(solution)/shard_map/ppermute | solution.py:27
  461.9 5.9 %collective-permute-start.55 = (f32[18,1]{1,0:T(8,128)S(1)}, f32[18,1]{1,0:T(8,128)S(1)}, u32[]{:S(2)}, u32[]{:S(2)}) collective-permute-start(f32[18,1]{1,0:T(8,128)S(1)} %get-tuple-element.95), channel_id=1, source_target_pairs={{0,1},{1,2},{2,3},{4,5},{5,6},{6,7},{8,9},{9,10},{10,11},{12,13},{... | collective-permute-start | bytes 224 | tf_op jit(solution)/shard_map/ppermute | solution.py:25
  501.3 5.8 %collective-permute-start.58 = (f32[18,1]{1,0:T(8,128)S(1)}, f32[18,1]{1,0:T(8,128)S(1)}, u32[]{:S(2)}, u32[]{:S(2)}) collective-permute-start(f32[18,1]{1,0:T(8,128)S(1)} %get-tuple-element.92), channel_id=1, source_target_pairs={{1,0},{2,1},{3,2},{5,4},{6,5},{7,6},{9,8},{10,9},{11,10},{13,12},{... | collective-permute-start | bytes 224 | tf_op jit(solution)/shard_map/ppermute | solution.py:27
  502.5 5.9 %collective-permute-start.59 = (f32[18,1]{1,0:T(8,128)S(1)}, f32[18,1]{1,0:T(8,128)S(1)}, u32[]{:S(2)}, u32[]{:S(2)}) collective-permute-start(f32[18,1]{1,0:T(8,128)S(1)} %get-tuple-element.93), channel_id=1, source_target_pairs={{0,1},{1,2},{2,3},{4,5},{5,6},{6,7},{8,9},{9,10},{10,11},{12,13},{... | collective-permute-start | bytes 224 | tf_op jit(solution)/shard_map/ppermute | solution.py:25
  545.4 5.8 %collective-permute-start.62 = (f32[18,1]{1,0:T(8,128)S(1)}, f32[18,1]{1,0:T(8,128)S(1)}, u32[]{:S(2)}, u32[]{:S(2)}) collective-permute-start(f32[18,1]{1,0:T(8,128)S(1)} %get-tuple-element.90), channel_id=1, source_target_pairs={{1,0},{2,1},{3,2},{5,4},{6,5},{7,6},{9,8},{10,9},{11,10},{13,12},{... | collective-permute-start | bytes 224 | tf_op jit(solution)/shard_map/ppermute | solution.py:27
  546.6 5.9 %collective-permute-start.63 = (f32[18,1]{1,0:T(8,128)S(1)}, f32[18,1]{1,0:T(8,128)S(1)}, u32[]{:S(2)}, u32[]{:S(2)}) collective-permute-start(f32[18,1]{1,0:T(8,128)S(1)} %get-tuple-element.91), channel_id=1, source_target_pairs={{0,1},{1,2},{2,3},{4,5},{5,6},{6,7},{8,9},{9,10},{10,11},{12,13},{... | collective-permute-start | bytes 224 | tf_op jit(solution)/shard_map/ppermute | solution.py:25
  (45 other events, 228.2 us)
